TPU v7x, 256 devices: a whole 4x4x8 slice. The times are simulated.
256 devices in a mesh: seq: 64 (over y_hi, z, x), rep: 4 (over y_lo, core).
Axes of the slice: x: 4, y: 4 (y_hi: 2, y_lo: 2; y = y_hi * 2 + y_lo), z: 8, core: 2. Of those that a mesh axis runs over, the one named last changes fastest.
Arguments:
- queries: bfloat16 [32768, 4096], P(('rep', 'seq')), parts along dimension 0, may hold values from -160 to 160
- keys_values: bfloat16 [2, 32768, 1024], P(None, ('rep', 'seq')), parts along dimension 1, may hold values from -6 to 6
- segment_ids: int32 [32768], P(('rep', 'seq')), parts along dimension 0, may hold values from 0 to 31, never falling along the last dimension, each value on 1 to 4096 neighbouring positions
Outputs:
- attended: bfloat16 [32768, 4096], P(('rep', 'seq')), parts along dimension 0
There are 4 independent parts, one for each index of `rep`. A program takes and returns all parts, laid end to end along the dimension named above; each array names one. Nothing has to cross between parts.
Inputs may be any that keep to these rules, and one draw needn't show every extreme that they name: `segment_ids`: ids never fall along the tokens; every document holds 1 to 4096 consecutive tokens, one exactly 4096.
All inputs are finite; a program needn't handle non-finite values.
Results may differ from a plain program's by a relative error of at most 0.004.
Values may be sent and summed in bfloat16 or wider, within the bound.
A program may use at most 192 MiB of HBM per device.

v0:
```python
import jax
import jax.numpy as jnp
from jax import lax
from jax.sharding import PartitionSpec as P

HQ = 32
HK = 8
DH = 128
WINDOW = 2048


NEG_BIG = -1e30


def passed_along(block, axis, distance):
    devices = range(lax.axis_size(axis))
    route = [(i - distance, i) for i in devices if i - distance in devices]
    return lax.ppermute(block, axis, route)


def local(queries, keys_values, segment_ids):
    shard_rows = queries.shape[0]
    group_size = HQ // HK
    score_scale = DH ** (-0.5)
    offset = lax.axis_index("seq") * shard_rows
    row_index = jnp.arange(shard_rows, dtype=jnp.int32)
    query_index = offset + row_index
    id_row = segment_ids.astype(jnp.bfloat16).reshape(1, shard_rows)
    query_ids = id_row[0]
    grouped = queries.reshape(shard_rows, HK, group_size, DH)
    own_block = (keys_values, id_row)

    def attend(running, block, key_first):
        run_max, run_sum, run_acc = running
        pair, key_ids = block
        key_block = pair[0].reshape(shard_rows, HK, DH)
        value_block = pair[1].reshape(shard_rows, HK, DH)
        scores = (
            jnp.einsum("qhgd,khd->hgqk", grouped, key_block, preferred_element_type=jnp.float32)
            * score_scale
        )
        key_index = key_first + row_index
        distance = query_index[:, None] - key_index[None, :]
        keep_mask = (
            (query_ids[:, None] == key_ids[0][None, :])
            & (distance >= 0)
            & (distance < WINDOW)
            & (key_index[None, :] >= 0)
        )
        scores = jnp.where(keep_mask, scores, NEG_BIG)
        new_max = jnp.maximum(run_max, jnp.max(scores, axis=-1))
        weights = jnp.where(keep_mask, jnp.exp(scores - new_max[..., None]), 0.0)
        rescale = jnp.exp(run_max - new_max)
        new_sum = run_sum * rescale + jnp.sum(weights, axis=-1)
        new_acc = run_acc * rescale[..., None] + jnp.einsum(
            "hgqk,khd->hgqd",
            weights.astype(jnp.bfloat16),
            value_block,
            preferred_element_type=jnp.float32,
        )
        return (new_max, new_sum, new_acc)

    def visit(running, block, key_first):
        return attend(running, block, key_first)

    initial = (
        jnp.full((HK, group_size, shard_rows), NEG_BIG, jnp.float32),
        jnp.zeros((HK, group_size, shard_rows), jnp.float32),
        jnp.zeros((HK, group_size, shard_rows, DH), jnp.float32),
    )
    blocks_total = WINDOW // shard_rows
    running = attend(initial, own_block, offset)

    def relay_step(shard_step, state):
        current, moving = state
        moving = passed_along((moving[0], moving[1]), "seq", 1)
        return (visit(current, moving, offset - shard_step * shard_rows), moving)

    running, leftover = lax.fori_loop(1, blocks_total + 1, relay_step, (running, own_block))
    run_max, run_sum, run_acc = running
    result = run_acc / run_sum[..., None]
    return jnp.transpose(result, (2, 0, 1, 3)).reshape(shard_rows, HQ * DH).astype(jnp.bfloat16)


def solution(mesh):
    return jax.shard_map(
        local,
        mesh=mesh,
        in_specs=(P(("rep", "seq"), None), P(None, ("rep", "seq"), None), P(("rep", "seq"))),
        out_specs=P(("rep", "seq"), None),
        check_vma=False,
    )
```

profile of v0, /device:TPU:24, one launch (start us, length us, event | category | flops | bytes accessed | tf_op | source)
XLA Modules:
  0.0 369.8 jit_solution(3821295212114971719)
XLA Ops:
  6.6 360.1 %while.23 = (s32[]{:T(128)}, f32[8,4,128]{2,1,0:T(4,128)S(1)}, f32[8,4,128]{2,1,0:T(4,128)S(1)}, f32[8,4,128,128]{3,2,1,0:T(8,128)S(1)}, bf16[2,128,1024]{1,2,0:...) while((s32[]{:T(128)}, f32[8,4,128]{2,1,0:T(4,128)S(1)}, ...), condition=%wide.region_5.6_spmd.clone.clone, body=%wide.region_2.5_spmd.clone.clone.sunk | while | flops 276455936 | bytes 16585185 | solution.py:79
  6.6 3.4 collective-permute-start.1
  10.0 3.4 collective-permute-start
  13.4 15.8 %collective-permute-done = bf16[1,128]{1,0:T(2,128)(2,1)S(1)} collective-permute-done((bf16[1,128]{1,0:T(2,128)(2,1)S(1)}, bf16[1,128]{1,0:T(2,128)(2,1)S(1)}, u32[]{:S(2)}, u32[]{:S(2)}) %collective-permute-start) | collective-permute-done | bytes 288 | tf_op jit(solution)/shard_map/while/body/eval_jaxpr/ppermute | solution.py:18
  37.7 16.8 %collective-permute-done = bf16[1,128]{1,0:T(2,128)(2,1)S(1)} collective-permute-done((bf16[1,128]{1,0:T(2,128)(2,1)S(1)}, bf16[1,128]{1,0:T(2,128)(2,1)S(1)}, u32[]{:S(2)}, u32[]{:S(2)}) %collective-permute-start) | collective-permute-done | bytes 288 | tf_op jit(solution)/shard_map/while/body/eval_jaxpr/ppermute | solution.py:18
  63.0 15.9 %collective-permute-done = bf16[1,128]{1,0:T(2,128)(2,1)S(1)} collective-permute-done((bf16[1,128]{1,0:T(2,128)(2,1)S(1)}, bf16[1,128]{1,0:T(2,128)(2,1)S(1)}, u32[]{:S(2)}, u32[]{:S(2)}) %collective-permute-start) | collective-permute-done | bytes 288 | tf_op jit(solution)/shard_map/while/body/eval_jaxpr/ppermute | solution.py:18
  81.4 2.0 multiply_add_fusion.5
  87.4 14.9 %collective-permute-done = bf16[1,128]{1,0:T(2,128)(2,1)S(1)} collective-permute-done((bf16[1,128]{1,0:T(2,128)(2,1)S(1)}, bf16[1,128]{1,0:T(2,128)(2,1)S(1)}, u32[]{:S(2)}, u32[]{:S(2)}) %collective-permute-start) | collective-permute-done | bytes 288 | tf_op jit(solution)/shard_map/while/body/eval_jaxpr/ppermute | solution.py:18
  104.9 2.0 multiply_add_fusion.5
  110.8 14.0 %collective-permute-done = bf16[1,128]{1,0:T(2,128)(2,1)S(1)} collective-permute-done((bf16[1,128]{1,0:T(2,128)(2,1)S(1)}, bf16[1,128]{1,0:T(2,128)(2,1)S(1)}, u32[]{:S(2)}, u32[]{:S(2)}) %collective-permute-start) | collective-permute-done | bytes 288 | tf_op jit(solution)/shard_map/while/body/eval_jaxpr/ppermute | solution.py:18
  127.3 2.0 multiply_add_fusion.5
  133.2 13.1 %collective-permute-done = bf16[1,128]{1,0:T(2,128)(2,1)S(1)} collective-permute-done((bf16[1,128]{1,0:T(2,128)(2,1)S(1)}, bf16[1,128]{1,0:T(2,128)(2,1)S(1)}, u32[]{:S(2)}, u32[]{:S(2)}) %collective-permute-start) | collective-permute-done | bytes 288 | tf_op jit(solution)/shard_map/while/body/eval_jaxpr/ppermute | solution.py:18
  154.8 13.0 %collective-permute-done = bf16[1,128]{1,0:T(2,128)(2,1)S(1)} collective-permute-done((bf16[1,128]{1,0:T(2,128)(2,1)S(1)}, bf16[1,128]{1,0:T(2,128)(2,1)S(1)}, u32[]{:S(2)}, u32[]{:S(2)}) %collective-permute-start) | collective-permute-done | bytes 288 | tf_op jit(solution)/shard_map/while/body/eval_jaxpr/ppermute | solution.py:18
  176.3 13.0 %collective-permute-done = bf16[1,128]{1,0:T(2,128)(2,1)S(1)} collective-permute-done((bf16[1,128]{1,0:T(2,128)(2,1)S(1)}, bf16[1,128]{1,0:T(2,128)(2,1)S(1)}, u32[]{:S(2)}, u32[]{:S(2)}) %collective-permute-start) | collective-permute-done | bytes 288 | tf_op jit(solution)/shard_map/while/body/eval_jaxpr/ppermute | solution.py:18
  197.7 13.0 %collective-permute-done = bf16[1,128]{1,0:T(2,128)(2,1)S(1)} collective-permute-done((bf16[1,128]{1,0:T(2,128)(2,1)S(1)}, bf16[1,128]{1,0:T(2,128)(2,1)S(1)}, u32[]{:S(2)}, u32[]{:S(2)}) %collective-permute-start) | collective-permute-done | bytes 288 | tf_op jit(solution)/shard_map/while/body/eval_jaxpr/ppermute | solution.py:18
  219.2 13.0 %collective-permute-done = bf16[1,128]{1,0:T(2,128)(2,1)S(1)} collective-permute-done((bf16[1,128]{1,0:T(2,128)(2,1)S(1)}, bf16[1,128]{1,0:T(2,128)(2,1)S(1)}, u32[]{:S(2)}, u32[]{:S(2)}) %collective-permute-start) | collective-permute-done | bytes 288 | tf_op jit(solution)/shard_map/while/body/eval_jaxpr/ppermute | solution.py:18
  240.7 13.0 %collective-permute-done = bf16[1,128]{1,0:T(2,128)(2,1)S(1)} collective-permute-done((bf16[1,128]{1,0:T(2,128)(2,1)S(1)}, bf16[1,128]{1,0:T(2,128)(2,1)S(1)}, u32[]{:S(2)}, u32[]{:S(2)}) %collective-permute-start) | collective-permute-done | bytes 288 | tf_op jit(solution)/shard_map/while/body/eval_jaxpr/ppermute | solution.py:18
  262.1 13.0 %collective-permute-done = bf16[1,128]{1,0:T(2,128)(2,1)S(1)} collective-permute-done((bf16[1,128]{1,0:T(2,128)(2,1)S(1)}, bf16[1,128]{1,0:T(2,128)(2,1)S(1)}, u32[]{:S(2)}, u32[]{:S(2)}) %collective-permute-start) | collective-permute-done | bytes 288 | tf_op jit(solution)/shard_map/while/body/eval_jaxpr/ppermute | solution.py:18
  283.6 13.0 %collective-permute-done = bf16[1,128]{1,0:T(2,128)(2,1)S(1)} collective-permute-done((bf16[1,128]{1,0:T(2,128)(2,1)S(1)}, bf16[1,128]{1,0:T(2,128)(2,1)S(1)}, u32[]{:S(2)}, u32[]{:S(2)}) %collective-permute-start) | collective-permute-done | bytes 288 | tf_op jit(solution)/shard_map/while/body/eval_jaxpr/ppermute | solution.py:18
  305.1 13.0 %collective-permute-done = bf16[1,128]{1,0:T(2,128)(2,1)S(1)} collective-permute-done((bf16[1,128]{1,0:T(2,128)(2,1)S(1)}, bf16[1,128]{1,0:T(2,128)(2,1)S(1)}, u32[]{:S(2)}, u32[]{:S(2)}) %collective-permute-start) | collective-permute-done | bytes 288 | tf_op jit(solution)/shard_map/while/body/eval_jaxpr/ppermute | solution.py:18
  326.6 14.0 %collective-permute-done = bf16[1,128]{1,0:T(2,128)(2,1)S(1)} collective-permute-done((bf16[1,128]{1,0:T(2,128)(2,1)S(1)}, bf16[1,128]{1,0:T(2,128)(2,1)S(1)}, u32[]{:S(2)}, u32[]{:S(2)}) %collective-permute-start) | collective-permute-done | bytes 288 | tf_op jit(solution)/shard_map/while/body/eval_jaxpr/ppermute | solution.py:18
  343.1 2.0 multiply_add_fusion.5
  349.1 13.0 %collective-permute-done = bf16[1,128]{1,0:T(2,128)(2,1)S(1)} collective-permute-done((bf16[1,128]{1,0:T(2,128)(2,1)S(1)}, bf16[1,128]{1,0:T(2,128)(2,1)S(1)}, u32[]{:S(2)}, u32[]{:S(2)}) %collective-permute-start) | collective-permute-done | bytes 288 | tf_op jit(solution)/shard_map/while/body/eval_jaxpr/ppermute | solution.py:18
  364.6 2.0 multiply_add_fusion.5
  (250 shorter events, 129.7 us)
Async XLA Ops:
  6.6 22.8 %collective-permute-start.1 = (bf16[2,128,1024]{1,2,0:T(8,128)(2,1)S(1)}, bf16[2,128,1024]{1,2,0:T(8,128)(2,1)S(1)}, u32[]{:S(2)}, u32[]{:S(2)}) collective-permute-start(bf16[2,128,1024]{1,2,0:T(8,128)(2,1)S(1)} %get-tuple-element.373), channel_id=1, source_target_pairs={{0,4},{4,8},{8,12},{12,16},{16,20},{20,24},{24,28},{28,32},{32,36}... | collective-permute-start | bytes 1572872 | tf_op jit(solution)/shard_map/while/body/eval_jaxpr/ppermute | solution.py:18
  10.0 19.2 %collective-permute-start = (bf16[1,128]{1,0:T(2,128)(2,1)S(1)}, bf16[1,128]{1,0:T(2,128)(2,1)S(1)}, u32[]{:S(2)}, u32[]{:S(2)}) collective-permute-start(bf16[1,128]{1,0:T(2,128)(2,1)S(1)} %get-tuple-element.374), channel_id=1, source_target_pairs={{0,4},{4,8},{8,12},{12,16},{16,20},{20,24},{24,28},{28,32},{32,36}... | collective-permute-start | bytes 776 | tf_op jit(solution)/shard_map/while/body/eval_jaxpr/ppermute | solution.py:18
  33.8 20.8 %collective-permute-start.1 = (bf16[2,128,1024]{1,2,0:T(8,128)(2,1)S(1)}, bf16[2,128,1024]{1,2,0:T(8,128)(2,1)S(1)}, u32[]{:S(2)}, u32[]{:S(2)}) collective-permute-start(bf16[2,128,1024]{1,2,0:T(8,128)(2,1)S(1)} %get-tuple-element.373), channel_id=1, source_target_pairs={{0,4},{4,8},{8,12},{12,16},{16,20},{20,24},{24,28},{28,32},{32,36}... | collective-permute-start | bytes 1572872 | tf_op jit(solution)/shard_map/while/body/eval_jaxpr/ppermute | solution.py:18
  35.7 18.8 %collective-permute-start = (bf16[1,128]{1,0:T(2,128)(2,1)S(1)}, bf16[1,128]{1,0:T(2,128)(2,1)S(1)}, u32[]{:S(2)}, u32[]{:S(2)}) collective-permute-start(bf16[1,128]{1,0:T(2,128)(2,1)S(1)} %get-tuple-element.374), channel_id=1, source_target_pairs={{0,4},{4,8},{8,12},{12,16},{16,20},{20,24},{24,28},{28,32},{32,36}... | collective-permute-start | bytes 776 | tf_op jit(solution)/shard_map/while/body/eval_jaxpr/ppermute | solution.py:18
  59.1 19.9 %collective-permute-start.1 = (bf16[2,128,1024]{1,2,0:T(8,128)(2,1)S(1)}, bf16[2,128,1024]{1,2,0:T(8,128)(2,1)S(1)}, u32[]{:S(2)}, u32[]{:S(2)}) collective-permute-start(bf16[2,128,1024]{1,2,0:T(8,128)(2,1)S(1)} %get-tuple-element.373), channel_id=1, source_target_pairs={{0,4},{4,8},{8,12},{12,16},{16,20},{20,24},{24,28},{28,32},{32,36}... | collective-permute-start | bytes 1572872 | tf_op jit(solution)/shard_map/while/body/eval_jaxpr/ppermute | solution.py:18
  61.0 17.8 %collective-permute-start = (bf16[1,128]{1,0:T(2,128)(2,1)S(1)}, bf16[1,128]{1,0:T(2,128)(2,1)S(1)}, u32[]{:S(2)}, u32[]{:S(2)}) collective-permute-start(bf16[1,128]{1,0:T(2,128)(2,1)S(1)} %get-tuple-element.374), channel_id=1, source_target_pairs={{0,4},{4,8},{8,12},{12,16},{16,20},{20,24},{24,28},{28,32},{32,36}... | collective-permute-start | bytes 776 | tf_op jit(solution)/shard_map/while/body/eval_jaxpr/ppermute | solution.py:18
  83.5 19.0 %collective-permute-start.1 = (bf16[2,128,1024]{1,2,0:T(8,128)(2,1)S(1)}, bf16[2,128,1024]{1,2,0:T(8,128)(2,1)S(1)}, u32[]{:S(2)}, u32[]{:S(2)}) collective-permute-start(bf16[2,128,1024]{1,2,0:T(8,128)(2,1)S(1)} %get-tuple-element.373), channel_id=1, source_target_pairs={{0,4},{4,8},{8,12},{12,16},{16,20},{20,24},{24,28},{28,32},{32,36}... | collective-permute-start | bytes 1572872 | tf_op jit(solution)/shard_map/while/body/eval_jaxpr/ppermute | solution.py:18
  85.4 16.9 %collective-permute-start = (bf16[1,128]{1,0:T(2,128)(2,1)S(1)}, bf16[1,128]{1,0:T(2,128)(2,1)S(1)}, u32[]{:S(2)}, u32[]{:S(2)}) collective-permute-start(bf16[1,128]{1,0:T(2,128)(2,1)S(1)} %get-tuple-element.374), channel_id=1, source_target_pairs={{0,4},{4,8},{8,12},{12,16},{16,20},{20,24},{24,28},{28,32},{32,36}... | collective-permute-start | bytes 776 | tf_op jit(solution)/shard_map/while/body/eval_jaxpr/ppermute | solution.py:18
  106.9 18.0 %collective-permute-start.1 = (bf16[2,128,1024]{1,2,0:T(8,128)(2,1)S(1)}, bf16[2,128,1024]{1,2,0:T(8,128)(2,1)S(1)}, u32[]{:S(2)}, u32[]{:S(2)}) collective-permute-start(bf16[2,128,1024]{1,2,0:T(8,128)(2,1)S(1)} %get-tuple-element.373), channel_id=1, source_target_pairs={{0,4},{4,8},{8,12},{12,16},{16,20},{20,24},{24,28},{28,32},{32,36}... | collective-permute-start | bytes 1572872 | tf_op jit(solution)/shard_map/while/body/eval_jaxpr/ppermute | solution.py:18
  108.8 16.0 %collective-permute-start = (bf16[1,128]{1,0:T(2,128)(2,1)S(1)}, bf16[1,128]{1,0:T(2,128)(2,1)S(1)}, u32[]{:S(2)}, u32[]{:S(2)}) collective-permute-start(bf16[1,128]{1,0:T(2,128)(2,1)S(1)} %get-tuple-element.374), channel_id=1, source_target_pairs={{0,4},{4,8},{8,12},{12,16},{16,20},{20,24},{24,28},{28,32},{32,36}... | collective-permute-start | bytes 776 | tf_op jit(solution)/shard_map/while/body/eval_jaxpr/ppermute | solution.py:18
  129.4 17.1 %collective-permute-start.1 = (bf16[2,128,1024]{1,2,0:T(8,128)(2,1)S(1)}, bf16[2,128,1024]{1,2,0:T(8,128)(2,1)S(1)}, u32[]{:S(2)}, u32[]{:S(2)}) collective-permute-start(bf16[2,128,1024]{1,2,0:T(8,128)(2,1)S(1)} %get-tuple-element.373), channel_id=1, source_target_pairs={{0,4},{4,8},{8,12},{12,16},{16,20},{20,24},{24,28},{28,32},{32,36}... | collective-permute-start | bytes 1572872 | tf_op jit(solution)/shard_map/while/body/eval_jaxpr/ppermute | solution.py:18
  131.3 15.0 %collective-permute-start = (bf16[1,128]{1,0:T(2,128)(2,1)S(1)}, bf16[1,128]{1,0:T(2,128)(2,1)S(1)}, u32[]{:S(2)}, u32[]{:S(2)}) collective-permute-start(bf16[1,128]{1,0:T(2,128)(2,1)S(1)} %get-tuple-element.374), channel_id=1, source_target_pairs={{0,4},{4,8},{8,12},{12,16},{16,20},{20,24},{24,28},{28,32},{32,36}... | collective-permute-start | bytes 776 | tf_op jit(solution)/shard_map/while/body/eval_jaxpr/ppermute | solution.py:18
  150.9 17.0 %collective-permute-start.1 = (bf16[2,128,1024]{1,2,0:T(8,128)(2,1)S(1)}, bf16[2,128,1024]{1,2,0:T(8,128)(2,1)S(1)}, u32[]{:S(2)}, u32[]{:S(2)}) collective-permute-start(bf16[2,128,1024]{1,2,0:T(8,128)(2,1)S(1)} %get-tuple-element.373), channel_id=1, source_target_pairs={{0,4},{4,8},{8,12},{12,16},{16,20},{20,24},{24,28},{28,32},{32,36}... | collective-permute-start | bytes 1572872 | tf_op jit(solution)/shard_map/while/body/eval_jaxpr/ppermute | solution.py:18
  152.8 15.0 %collective-permute-start = (bf16[1,128]{1,0:T(2,128)(2,1)S(1)}, bf16[1,128]{1,0:T(2,128)(2,1)S(1)}, u32[]{:S(2)}, u32[]{:S(2)}) collective-permute-start(bf16[1,128]{1,0:T(2,128)(2,1)S(1)} %get-tuple-element.374), channel_id=1, source_target_pairs={{0,4},{4,8},{8,12},{12,16},{16,20},{20,24},{24,28},{28,32},{32,36}... | collective-permute-start | bytes 776 | tf_op jit(solution)/shard_map/while/body/eval_jaxpr/ppermute | solution.py:18
  172.4 17.0 %collective-permute-start.1 = (bf16[2,128,1024]{1,2,0:T(8,128)(2,1)S(1)}, bf16[2,128,1024]{1,2,0:T(8,128)(2,1)S(1)}, u32[]{:S(2)}, u32[]{:S(2)}) collective-permute-start(bf16[2,128,1024]{1,2,0:T(8,128)(2,1)S(1)} %get-tuple-element.373), channel_id=1, source_target_pairs={{0,4},{4,8},{8,12},{12,16},{16,20},{20,24},{24,28},{28,32},{32,36}... | collective-permute-start | bytes 1572872 | tf_op jit(solution)/shard_map/while/body/eval_jaxpr/ppermute | solution.py:18
  193.8 17.0 %collective-permute-start.1 = (bf16[2,128,1024]{1,2,0:T(8,128)(2,1)S(1)}, bf16[2,128,1024]{1,2,0:T(8,128)(2,1)S(1)}, u32[]{:S(2)}, u32[]{:S(2)}) collective-permute-start(bf16[2,128,1024]{1,2,0:T(8,128)(2,1)S(1)} %get-tuple-element.373), channel_id=1, source_target_pairs={{0,4},{4,8},{8,12},{12,16},{16,20},{20,24},{24,28},{28,32},{32,36}... | collective-permute-start | bytes 1572872 | tf_op jit(solution)/shard_map/while/body/eval_jaxpr/ppermute | solution.py:18
  215.3 17.0 %collective-permute-start.1 = (bf16[2,128,1024]{1,2,0:T(8,128)(2,1)S(1)}, bf16[2,128,1024]{1,2,0:T(8,128)(2,1)S(1)}, u32[]{:S(2)}, u32[]{:S(2)}) collective-permute-start(bf16[2,128,1024]{1,2,0:T(8,128)(2,1)S(1)} %get-tuple-element.373), channel_id=1, source_target_pairs={{0,4},{4,8},{8,12},{12,16},{16,20},{20,24},{24,28},{28,32},{32,36}... | collective-permute-start | bytes 1572872 | tf_op jit(solution)/shard_map/while/body/eval_jaxpr/ppermute | solution.py:18
  236.8 17.0 %collective-permute-start.1 = (bf16[2,128,1024]{1,2,0:T(8,128)(2,1)S(1)}, bf16[2,128,1024]{1,2,0:T(8,128)(2,1)S(1)}, u32[]{:S(2)}, u32[]{:S(2)}) collective-permute-start(bf16[2,128,1024]{1,2,0:T(8,128)(2,1)S(1)} %get-tuple-element.373), channel_id=1, source_target_pairs={{0,4},{4,8},{8,12},{12,16},{16,20},{20,24},{24,28},{28,32},{32,36}... | collective-permute-start | bytes 1572872 | tf_op jit(solution)/shard_map/while/body/eval_jaxpr/ppermute | solution.py:18
  258.3 17.0 %collective-permute-start.1 = (bf16[2,128,1024]{1,2,0:T(8,128)(2,1)S(1)}, bf16[2,128,1024]{1,2,0:T(8,128)(2,1)S(1)}, u32[]{:S(2)}, u32[]{:S(2)}) collective-permute-start(bf16[2,128,1024]{1,2,0:T(8,128)(2,1)S(1)} %get-tuple-element.373), channel_id=1, source_target_pairs={{0,4},{4,8},{8,12},{12,16},{16,20},{20,24},{24,28},{28,32},{32,36}... | collective-permute-start | bytes 1572872 | tf_op jit(solution)/shard_map/while/body/eval_jaxpr/ppermute | solution.py:18
  279.7 17.0 %collective-permute-start.1 = (bf16[2,128,1024]{1,2,0:T(8,128)(2,1)S(1)}, bf16[2,128,1024]{1,2,0:T(8,128)(2,1)S(1)}, u32[]{:S(2)}, u32[]{:S(2)}) collective-permute-start(bf16[2,128,1024]{1,2,0:T(8,128)(2,1)S(1)} %get-tuple-element.373), channel_id=1, source_target_pairs={{0,4},{4,8},{8,12},{12,16},{16,20},{20,24},{24,28},{28,32},{32,36}... | collective-permute-start | bytes 1572872 | tf_op jit(solution)/shard_map/while/body/eval_jaxpr/ppermute | solution.py:18
  301.2 17.0 %collective-permute-start.1 = (bf16[2,128,1024]{1,2,0:T(8,128)(2,1)S(1)}, bf16[2,128,1024]{1,2,0:T(8,128)(2,1)S(1)}, u32[]{:S(2)}, u32[]{:S(2)}) collective-permute-start(bf16[2,128,1024]{1,2,0:T(8,128)(2,1)S(1)} %get-tuple-element.373), channel_id=1, source_target_pairs={{0,4},{4,8},{8,12},{12,16},{16,20},{20,24},{24,28},{28,32},{32,36}... | collective-permute-start | bytes 1572872 | tf_op jit(solution)/shard_map/while/body/eval_jaxpr/ppermute | solution.py:18
  322.7 18.0 %collective-permute-start.1 = (bf16[2,128,1024]{1,2,0:T(8,128)(2,1)S(1)}, bf16[2,128,1024]{1,2,0:T(8,128)(2,1)S(1)}, u32[]{:S(2)}, u32[]{:S(2)}) collective-permute-start(bf16[2,128,1024]{1,2,0:T(8,128)(2,1)S(1)} %get-tuple-element.373), channel_id=1, source_target_pairs={{0,4},{4,8},{8,12},{12,16},{16,20},{20,24},{24,28},{28,32},{32,36}... | collective-permute-start | bytes 1572872 | tf_op jit(solution)/shard_map/while/body/eval_jaxpr/ppermute | solution.py:18
  324.6 16.0 %collective-permute-start = (bf16[1,128]{1,0:T(2,128)(2,1)S(1)}, bf16[1,128]{1,0:T(2,128)(2,1)S(1)}, u32[]{:S(2)}, u32[]{:S(2)}) collective-permute-start(bf16[1,128]{1,0:T(2,128)(2,1)S(1)} %get-tuple-element.374), channel_id=1, source_target_pairs={{0,4},{4,8},{8,12},{12,16},{16,20},{20,24},{24,28},{28,32},{32,36}... | collective-permute-start | bytes 776 | tf_op jit(solution)/shard_map/while/body/eval_jaxpr/ppermute | solution.py:18
  345.2 17.0 %collective-permute-start.1 = (bf16[2,128,1024]{1,2,0:T(8,128)(2,1)S(1)}, bf16[2,128,1024]{1,2,0:T(8,128)(2,1)S(1)}, u32[]{:S(2)}, u32[]{:S(2)}) collective-permute-start(bf16[2,128,1024]{1,2,0:T(8,128)(2,1)S(1)} %get-tuple-element.373), channel_id=1, source_target_pairs={{0,4},{4,8},{8,12},{12,16},{16,20},{20,24},{24,28},{28,32},{32,36}... | collective-permute-start | bytes 1572872 | tf_op jit(solution)/shard_map/while/body/eval_jaxpr/ppermute | solution.py:18
  (9 other events, 121.9 us)
where the time goes:
time: 371 us; the launch traced here: 370 us
  waiting for transfers between devices  222 us (60%)
  starting transfers between devices  64.4 us (17%)
  matrix products  61.2 us (16%)
  other arithmetic  13.6 us (4%)
  local copies, waits for them, and re-layouts  7 us (2%)
    ppermute x32, waiting for transfers between devices, passed_along(): return lax.ppermute(block, axis, route)  222 us
    ppermute x32, starting transfers between devices, passed_along(): return lax.ppermute(block, axis, route)  64.4 us
    dot_general x17, matrix products, attend(): jnp.einsum('hgqk,khd->hgqd', weights.astype(jnp.bfloat16), value_block, p...  32.6 us
    dot_general x17, matrix products, attend(): jnp.einsum('qhgd,khd->hgqk', grouped, key_block, preferred_element_type=j...  28.6 us
    reduce_sum x17, other arithmetic, attend(): new_sum = run_sum * rescale + jnp.sum(weights, axis=-1)  9.65 us
  transfers between devices with their start and end apart: 32, of which 16 were waited for; matrix products, arithmetic and copies ran while one was open for 1% of the time, Pallas kernels for 0%

commit v1 on v0

v1 whole, which is shorter than its diff:
```python
import math

import jax
import jax.numpy as jnp
from jax import lax
from jax.experimental import pallas as pl
from jax.experimental.pallas import tpu as pltpu
from jax.sharding import PartitionSpec as P

HQ = 32
HK = 8
DH = 128
WINDOW = 2048

RING = 4
ROWS = 128
PLANE = RING * ROWS
SLOTS = WINDOW // PLANE + 1
GROUP = HQ // HK
HEADS = HK // RING
WIDE = GROUP * DH
NEG_BIG = -1e30
SCALE = DH**-0.5 * math.log2(math.e)
MESH = pl.DeviceIdType.MESH


def kernel(
    q_hbm, kv_hbm, id_in, o_hbm,
    qbuf, kvb, idb, qidc, m_sc, l_sc, acc_sc, obuf,
    loc_sem, kvx_ss, kv_rs, z_ss, qx_ss, q_rs, idx_ss, id0_rs, idz_ss, idz_rs, o_ss, o_rs,
):
    planes = lax.axis_size("seq") // RING
    me = lax.axis_index("seq")
    x = lax.rem(me, RING)
    plane = me // RING
    has_next = plane < planes - 1
    has_prev = plane > 0
    ring_base = plane * RING
    nxt = lax.rem(me + RING, planes * RING)
    prv = lax.rem(me + (planes - 1) * RING, planes * RING)

    def partner(d):
        return lax.rem(x + d, RING)

    def remote(src, dst, ss, rs, seq):
        return pltpu.make_async_remote_copy(
            src_ref=src, dst_ref=dst, send_sem=ss, recv_sem=rs,
            device_id={"seq": seq}, device_id_type=MESH,
        )

    def kv_src(px, a):
        return kv_hbm.at[:, :, pl.ds(pl.multiple_of((px * HEADS + a) * DH, DH), DH)]

    def q_src(px, a):
        return q_hbm.at[:, pl.ds(pl.multiple_of((px * HEADS + a) * WIDE, WIDE), WIDE)]

    def chunk(a, slot, c):
        return kvb.at[a, slot, :, pl.ds(pl.multiple_of(c * ROWS, ROWS), ROWS), :]

    local = []
    for a in range(HEADS):
        local.append(pltpu.make_async_copy(kv_src(x, a), chunk(a, 0, x), loc_sem.at[a]))
        local.append(pltpu.make_async_copy(q_src(x, a), qbuf.at[a, x], loc_sem.at[HEADS + a]))
    for cp in local:
        cp.start()
    idb[0, x] = id_in[...]

    barrier = pltpu.get_barrier_semaphore()
    for d in range(1, RING):
        pl.semaphore_signal(barrier, inc=1, device_id={"seq": ring_base + partner(d)}, device_id_type=MESH)

    @pl.when(has_prev)
    def _():
        pl.semaphore_signal(barrier, inc=1, device_id={"seq": prv}, device_id_type=MESH)

    @pl.when(has_next)
    def _():
        pl.semaphore_wait(barrier, RING)

    @pl.when(jnp.logical_not(has_next))
    def _():
        pl.semaphore_wait(barrier, RING - 1)

    def id_send(d):
        return remote(id_in, idb.at[0, x], idx_ss.at[d - 1], id0_rs.at[x], ring_base + partner(d))

    def kv_send(a, d):
        px = partner(d)
        return remote(kv_src(px, a), chunk(a, 0, x), kvx_ss.at[a, d - 1], kv_rs.at[a, 0, x], ring_base + px)

    def q_send(a, d):
        px = partner(d)
        return remote(q_src(px, a), qbuf.at[a, x], qx_ss.at[a, d - 1], q_rs.at[a, x], ring_base + px)

    def own_forward(a):
        return remote(kv_src(x, a), chunk(a, 1, x), z_ss.at[a, 0, x], kv_rs.at[a, 1, x], nxt)

    def forward(a, slot, c):
        return remote(chunk(a, slot, c), chunk(a, slot + 1, c), z_ss.at[a, slot, c], kv_rs.at[a, slot + 1, c], nxt)

    def id_forward(slot):
        return remote(idb.at[slot], idb.at[slot + 1], idz_ss.at[slot], idz_rs.at[slot + 1], nxt)

    def arrived(a, slot, c):
        return remote(chunk(a, slot, c), chunk(a, slot, c), kvx_ss.at[0, 0], kv_rs.at[a, slot, c], nxt)

    @pl.when(has_next)
    def _():
        own_forward(0).start()

    for d in range(1, RING):
        id_send(d).start()
    for d in range(1, RING):
        kv_send(0, d).start()
    for d in range(1, RING):
        q_send(0, d).start()
    for a in range(1, HEADS):
        for d in range(1, RING):
            kv_send(a, d).start()
        for d in range(1, RING):
            q_send(a, d).start()

    def receive(e):
        step, j = e // RING, lax.rem(e, RING)
        a, slot = step // SLOTS, lax.rem(step, SLOTS)
        c = lax.rem(x + j, RING)

        @pl.when(jnp.logical_and(a == 0, j == 0))
        def _():
            @pl.when(slot == 0)
            def _():
                for d in range(1, RING):
                    pc = partner(d)
                    remote(idb.at[0, pc], idb.at[0, pc], idx_ss.at[0], id0_rs.at[pc], nxt).wait_recv()

            @pl.when(jnp.logical_and(slot > 0, slot <= plane))
            def _():
                remote(idb.at[slot], idb.at[slot], idx_ss.at[0], idz_rs.at[slot], nxt).wait_recv()

            @pl.when(jnp.logical_and(has_next, jnp.logical_and(slot <= plane, slot < SLOTS - 1)))
            def _():
                id_forward(slot).start()

        @pl.when(jnp.logical_and(slot == 0, j == 0))
        def _():
            pltpu.make_async_copy(kv_src(x, a), chunk(a, 0, x), loc_sem.at[a]).wait()

            @pl.when(jnp.logical_and(has_next, a > 0))
            def _():
                own_forward(a).start()

        @pl.when(jnp.logical_and(slot <= plane, jnp.logical_or(slot > 0, j > 0)))
        def _():
            arrived(a, slot, c).wait_recv()

            @pl.when(jnp.logical_and(has_next, slot < SLOTS - 1))
            def _():
                forward(a, slot, c).start()

    row = lax.broadcasted_iota(jnp.int32, (ROWS, ROWS), 0)
    col = lax.broadcasted_iota(jnp.int32, (ROWS, ROWS), 1)

    def piece(n):
        step, j = n // RING, lax.rem(n, RING)
        a, slot = step // SLOTS, lax.rem(step, SLOTS)
        qb = lax.rem(x + 1 + j, RING)

        @pl.when(slot == 0)
        def _():
            @pl.when(j < RING - 1)
            def _():
                remote(qbuf.at[a, qb], qbuf.at[a, qb], idx_ss.at[0], q_rs.at[a, qb], nxt).wait_recv()

            @pl.when(j == RING - 1)
            def _():
                pltpu.make_async_copy(q_src(x, a), qbuf.at[a, x], loc_sem.at[HEADS + a]).wait()

            m_sc[qb] = jnp.full((GROUP * ROWS, DH), NEG_BIG, jnp.float32)
            l_sc[qb] = jnp.zeros((GROUP * ROWS, DH), jnp.float32)
            acc_sc[qb] = jnp.zeros((GROUP * ROWS, DH), jnp.float32)
            qidc[qb] = jnp.transpose(jnp.broadcast_to(idb[0, qb], (ROWS, ROWS)))

        @pl.when(slot <= plane)
        def _():
            query_ids = qidc[qb]
            bias = []
            for c in range(RING):
                distance = row - col + (slot * PLANE + (qb - c) * ROWS)
                keep = (query_ids == idb[slot, c]) & (distance >= 0) & (distance < WINDOW)
                bias.append(jnp.where(keep, 0.0, NEG_BIG))
            bias = jnp.concatenate(bias, axis=1)
            q_all = qbuf[a, qb]
            q4 = jnp.concatenate([q_all[:, g * DH : (g + 1) * DH] for g in range(GROUP)], axis=0)
            keys = kvb[a, slot, 0]
            values = kvb[a, slot, 1]
            s = lax.dot_general(q4, keys, (((1,), (1,)), ((), ())), preferred_element_type=jnp.float32)
            s = s + jnp.concatenate([bias] * GROUP, axis=0)
            m_prev = m_sc[qb]
            m_new = jnp.maximum(m_prev, jnp.max(s, axis=1, keepdims=True))
            alpha = jnp.exp2((m_prev - m_new) * SCALE)
            p = jnp.exp2((s - jnp.concatenate([m_new] * RING, axis=1)) * SCALE)
            part = p[:, :ROWS]
            for c in range(1, RING):
                part = part + p[:, c * ROWS : (c + 1) * ROWS]
            l_sc[qb] = l_sc[qb] * alpha + part
            acc_sc[qb] = acc_sc[qb] * alpha + jnp.dot(
                p.astype(jnp.bfloat16), values, preferred_element_type=jnp.float32
            )
            m_sc[qb] = m_new

        @pl.when(slot == SLOTS - 1)
        def _():
            out = acc_sc[qb] / jnp.sum(l_sc[qb], axis=1, keepdims=True)
            for g in range(GROUP):
                obuf[a, qb, :, g * DH : (g + 1) * DH] = out[g * ROWS : (g + 1) * ROWS].astype(jnp.bfloat16)

            @pl.when(j < RING - 1)
            def _():
                o_send(a, qb).start()

            @pl.when(j == RING - 1)
            def _():
                o_local(a).start()

    def o_dst(px, a):
        return o_hbm.at[:, pl.ds(pl.multiple_of((px * HEADS + a) * WIDE, WIDE), WIDE)]

    def o_send(a, qb):
        return remote(obuf.at[a, qb], o_dst(x, a), o_ss.at[a, qb], o_rs.at[a, x], ring_base + qb)

    def o_local(a):
        return pltpu.make_async_copy(obuf.at[a, x], o_dst(x, a), loc_sem.at[2 * HEADS + a])

    events = HEADS * SLOTS * RING

    def done(e):
        return jnp.maximum(0, jnp.minimum(2 * (e - 7), e - 3))

    def event(e, carry):
        receive(e)

        def inner(n, c):
            piece(n)
            return c

        lax.fori_loop(done(e - 1), done(e), inner, 0)
        return carry

    lax.fori_loop(0, events, event, 0)

    def tail(n, c):
        piece(n)
        return c

    lax.fori_loop(events - RING, events, tail, 0)

    for a in range(HEADS):
        for d in range(1, RING):
            kv_send(a, d).wait_send()
            q_send(a, d).wait_send()
            pc = partner(d)
            o_send(a, pc).wait_send()
            remote(o_dst(pc, a), o_dst(pc, a), idx_ss.at[0], o_rs.at[a, pc], nxt).wait_recv()
        o_local(a).wait()
    for d in range(1, RING):
        id_send(d).wait_send()

    @pl.when(has_next)
    def _():
        def drain(n, c):
            a, k = n // (RING * (SLOTS - 1)), lax.rem(n, RING * (SLOTS - 1))
            slot, cc = k // RING, lax.rem(k, RING)

            @pl.when(slot <= plane)
            def _():
                forward(a, slot, cc).wait_send()

            return c

        lax.fori_loop(0, HEADS * RING * (SLOTS - 1), drain, 0)
        for slot in range(SLOTS - 1):
            @pl.when(slot <= plane)
            def _():
                id_forward(slot).wait_send()


def local(queries, keys_values, segment_ids):
    dma = pltpu.SemaphoreType.DMA
    return pl.pallas_call(
        kernel,
        out_shape=jax.ShapeDtypeStruct(queries.shape, queries.dtype),
        in_specs=[
            pl.BlockSpec(memory_space=pl.ANY),
            pl.BlockSpec(memory_space=pl.ANY),
            pl.BlockSpec(memory_space=pltpu.VMEM),
        ],
        out_specs=pl.BlockSpec(memory_space=pl.ANY),
        scratch_shapes=[
            pltpu.VMEM((HEADS, RING, ROWS, WIDE), jnp.bfloat16),
            pltpu.VMEM((HEADS, SLOTS, 2, PLANE, DH), jnp.bfloat16),
            pltpu.VMEM((SLOTS, RING, 1, ROWS), jnp.int32),
            pltpu.VMEM((RING, ROWS, ROWS), jnp.int32),
            pltpu.VMEM((RING, GROUP * ROWS, DH), jnp.float32),
            pltpu.VMEM((RING, GROUP * ROWS, DH), jnp.float32),
            pltpu.VMEM((RING, GROUP * ROWS, DH), jnp.float32),
            pltpu.VMEM((HEADS, RING, ROWS, WIDE), jnp.bfloat16),
            dma((3 * HEADS,)),
            dma((HEADS, RING - 1)),
            dma((HEADS, SLOTS, RING)),
            dma((HEADS, SLOTS - 1, RING)),
            dma((HEADS, RING - 1)),
            dma((HEADS, RING)),
            dma((RING - 1,)),
            dma((RING,)),
            dma((SLOTS - 1,)),
            dma((SLOTS,)),
            dma((HEADS, RING)),
            dma((HEADS, RING)),
        ],
        compiler_params=pltpu.CompilerParams(collective_id=0, has_side_effects=True),
        name="window_attention",
    )(queries, keys_values, segment_ids.reshape(1, ROWS))


def solution(mesh):
    return jax.shard_map(
        local,
        mesh=mesh,
        in_specs=(P(("rep", "seq"), None), P(None, ("rep", "seq"), None), P(("rep", "seq"))),
        out_specs=P(("rep", "seq"), None),
        check_vma=False,
    )
```

time: 371 us -> 72.6 us (0.20)
  waiting for transfers between devices: 222 us -> 0 us
  Pallas kernels: 0 us -> 69.8 us
  starting transfers between devices: 64.4 us -> 0 us
  matrix products: 61.2 us -> 0 us
  other arithmetic: 13.6 us -> 0 us
  local copies, waits for them, and re-layouts: 7 us -> 2.29 us
    ppermute x32 -> x0, waiting for transfers between devices: 222 us -> none  [passed_along(): return lax.ppermute(block, axis, route)]
    pallas_call x0 -> x1, Pallas kernels: none -> 69.8 us  [local(): pl.pallas_call(kernel, out_shape=jax.ShapeDtypeStruct(queries.shape, quer...]
    ppermute x32 -> x0, starting transfers between devices: 64.4 us -> none  [passed_along(): return lax.ppermute(block, axis, route)]
    dot_general x34 -> x0, matrix products: 61.2 us -> none  [the longest x17 32.6 us: attend(): jnp.einsum('hgqk,khd->hgqd', weights.astype(jnp.bfloat16), value_block, p...]
    reduce_sum x17 -> x0, other arithmetic: 9.65 us -> none  [attend(): new_sum = run_sum * rescale + jnp.sum(weights, axis=-1)]
  transfers between devices with their start and end apart: 32 -> 0, of which waited for: 16 -> 0; matrix products, arithmetic and copies ran while one was open for 1% -> 0% of each run, Pallas kernels for 0% -> 0%
where the time goes in v1:
time: 72.6 us; the launch traced here: 72.1 us
  Pallas kernels  69.8 us (96%)
  local copies, waits for them, and re-layouts  2.29 us (3%)
    pallas_call x1, Pallas kernels, local(): pl.pallas_call(kernel, out_shape=jax.ShapeDtypeStruct(queries.shape, quer...  69.8 us
    unnamed x1, local copies, waits for them, and re-layouts  2.29 us

profile of v1, /device:TPU:24, one launch (start us, length us, event | category | flops | bytes accessed | tf_op | source)
XLA Modules:
  0.0 72.1 jit_solution(659432254518945084)
XLA Ops:
  0.0 69.8 %window_attention.1 = bf16[128,4096]{1,0:T(8,128)(2,1)} custom-call(bf16[128,4096]{1,0:T(8,128)(2,1)} %q_hbm.1, bf16[2,128,1024]{2,1,0:T(8,128)(2,1)} %kv_hbm.1, s32[1,128]{1,0:T(1,128)} %bitcast.1), custom_call_target="tpu_custom_call" | custom-call | tf_op jit(solution)/shard_map/window_attention/pallas_call | solution.py:289
  69.8 2.3 %copy.5 = bf16[128,4096]{1,0:T(8,128)(2,1)} copy(bf16[128,4096]{1,0:T(8,128)(2,1)} %window_attention.1) | data formatting | bytes 2097152

commit v2 on v1

v2 whole, which is shorter than its diff:
```python
import math

import jax
import jax.numpy as jnp
from jax import lax
from jax.experimental import pallas as pl
from jax.experimental.pallas import tpu as pltpu
from jax.sharding import PartitionSpec as P

HQ = 32
HK = 8
DH = 128
WINDOW = 2048

RING = 4
ROWS = 128
PLANE = RING * ROWS
SLOTS = WINDOW // PLANE + 1
GROUP = HQ // HK
HEADS = HK // RING
WIDE = GROUP * DH
NEG_BIG = -1e30
SCALE = DH**-0.5 * math.log2(math.e)
MESH = pl.DeviceIdType.MESH
ZRING = 8
PLANES = 16
BACK = HEADS - 1
BACKS = RING - 1
LAST_BACK = PLANES - 3
F_EVENTS = 24
R_LAG = 4
R_EARLY = 4
R_LATE = 4


def kernel(
    q_hbm, kv_hbm, id_in, o_hbm,
    qbuf, kvb, rel, idb, qidc, m_sc, l_sc, acc_sc, obuf,
    loc_sem, kvx_ss, kv_rs, z_ss, qx_ss, q_rs, idx_ss, id0_rs, idz_ss, idz_rs, o_ss, o_rs,
    back_ss, rel_ss, rel_rs, rz_ss, ext, ext_ss, ext_rs,
):
    me = lax.axis_index("seq")
    x = lax.rem(me, RING)
    plane = me // RING
    half = plane // ZRING
    z = lax.rem(plane, ZRING)
    has_next = plane < PLANES - 1
    ring_base = plane * RING
    nxt = lax.rem(me + RING, PLANES * RING)
    prv = lax.rem(me + (PLANES - 1) * RING, PLANES * RING)

    def around(k):
        return half * ZRING + lax.rem(z + k, ZRING)

    down = around(ZRING - 1) * RING + x
    up = around(1) * RING + x

    def partner(d):
        return lax.rem(x + d, RING)

    def remote(src, dst, ss, rs, seq):
        return pltpu.make_async_remote_copy(
            src_ref=src, dst_ref=dst, send_sem=ss, recv_sem=rs,
            device_id={"seq": seq}, device_id_type=MESH,
        )

    def kv_src(px, a):
        return kv_hbm.at[:, :, pl.ds(pl.multiple_of((px * HEADS + a) * DH, DH), DH)]

    def q_src(px, a):
        return q_hbm.at[:, pl.ds(pl.multiple_of((px * HEADS + a) * WIDE, WIDE), WIDE)]

    def o_dst(px, a):
        return o_hbm.at[:, pl.ds(pl.multiple_of((px * HEADS + a) * WIDE, WIDE), WIDE)]

    def rows(c):
        return pl.ds(c * ROWS if isinstance(c, int) else pl.multiple_of(c * ROWS, ROWS), ROWS)

    def chunk(a, slot, c):
        return kvb.at[a, slot, :, rows(c), :]

    def signal(sem, seq):
        pl.semaphore_signal(sem, inc=1, device_id={"seq": seq}, device_id_type=MESH)

    def when(cond):
        return pl.when(cond)

    kv_local = [pltpu.make_async_copy(kv_src(x, a), chunk(a, 0, x), loc_sem.at[a]) for a in range(HEADS)]
    q_local = [pltpu.make_async_copy(q_src(x, a), qbuf.at[a, x], loc_sem.at[HEADS + a]) for a in range(HEADS)]
    for cp in kv_local + q_local:
        cp.start()
    idb[0, x] = id_in[...]

    barrier = pltpu.get_barrier_semaphore()
    third = around(3)
    for d in range(1, RING):
        signal(barrier, ring_base + partner(d))
    signal(barrier, up)

    @when(plane > 0)
    def _():
        signal(barrier, prv)

    def last_relay(source):
        h = source // ZRING
        return (h * ZRING + lax.rem(source + ZRING - 3, ZRING)) * RING + x

    @when(plane >= SLOTS - 1)
    def _():
        signal(barrier, last_relay(plane - (SLOTS - 1)))

    @when(plane == PLANES - 1)
    def _():
        signal(barrier, last_relay(PLANES - 4))
        signal(barrier, last_relay(PLANES - 3))

    @when(jnp.logical_and(jnp.logical_and(plane >= 2, plane != ZRING - 1), has_next))
    def _():
        signal(barrier, nxt)

    targets = (has_next, third <= LAST_BACK, jnp.logical_and(plane >= 3, plane != ZRING))
    count = jnp.int32(RING)
    for target in targets:
        count = count + jnp.where(target, 1, 0)
    pl.semaphore_wait(barrier, count)

    def id_send(d):
        return remote(id_in, idb.at[0, x], idx_ss.at[d - 1], id0_rs.at[x], ring_base + partner(d))

    def kv_send(a, d):
        px = partner(d)
        return remote(kv_src(px, a), chunk(a, 0, x), kvx_ss.at[a, d - 1], kv_rs.at[a, 0, x], ring_base + px)

    def q_send(a, d):
        px = partner(d)
        return remote(q_src(px, a), qbuf.at[a, x], qx_ss.at[a, d - 1], q_rs.at[a, x], ring_base + px)

    def own_forward(a):
        return remote(kv_src(x, a), chunk(a, 1, x), z_ss.at[a, 0, x], kv_rs.at[a, 1, x], nxt)

    def forward(a, slot, c):
        return remote(chunk(a, slot, c), chunk(a, slot + 1, c), z_ss.at[a, slot, c], kv_rs.at[a, slot + 1, c], nxt)

    def id_forward(slot):
        return remote(idb.at[slot], idb.at[slot + 1], idz_ss.at[slot], idz_rs.at[slot + 1], nxt)

    def wait_chunk(a, slot, c):
        remote(chunk(a, slot, c), chunk(a, slot, c), kvx_ss.at[0, 0], kv_rs.at[a, slot, c], nxt).wait_recv()

    def back_own(k):
        return remote(chunk(BACK, 0, k + 1), rel.at[0, k], back_ss.at[k], rel_rs.at[0, k], down)

    def back_relay(i, k):
        if i < 2:
            return remote(rel.at[i, k], rel.at[i + 1, k], rel_ss.at[i, k], rel_rs.at[i + 1, k], down)
        over = jnp.maximum(third - (PLANES - SLOTS), 0)
        slot = SLOTS - 1 - over
        first = jnp.minimum(third + SLOTS - 1, PLANES - 1) * RING + x
        return remote(rel.at[i, k], chunk(BACK, slot, k + 1), rel_ss.at[i, k], kv_rs.at[BACK, slot, k + 1], first)

    def back_next(slot, k):
        return remote(
            chunk(BACK, slot, k + 1), chunk(BACK, slot - 1, k + 1),
            rz_ss.at[slot - 3, k], kv_rs.at[BACK, slot - 1, k + 1], prv,
        )

    def ext_down(e, k, src):
        return remote(src, ext.at[e, k], ext_ss.at[e, k], ext_rs.at[e, k], down)

    def ext_last(e, k):
        slot = 3 - e
        return remote(ext.at[e, k], chunk(BACK, slot, k + 1), ext_ss.at[e, k], kv_rs.at[BACK, slot, k + 1], down)

    def wait_ext(e, k):
        remote(ext.at[e, k], ext.at[e, k], idx_ss.at[0], ext_rs.at[e, k], nxt).wait_recv()

    def o_send(a, qb):
        return remote(obuf.at[a, qb], o_dst(x, a), o_ss.at[a, qb], o_rs.at[a, x], ring_base + qb)

    def o_local(a):
        return pltpu.make_async_copy(obuf.at[a, x], o_dst(x, a), loc_sem.at[2 * HEADS + a])

    @when(has_next)
    def _():
        for a in range(HEADS):
            own_forward(a).start()

    for d in range(1, RING):
        id_send(d).start()
    for a in range(HEADS):
        for d in (1, 3, 2):
            kv_send(a, d).start()
    for a in range(HEADS):
        for d in (1, 3, 2):
            q_send(a, d).start()

    kv_local[0].wait()
    for j in (1, 3, 2):
        wait_chunk(0, 0, partner(j))

        @when(has_next)
        def _():
            forward(0, 0, partner(j)).start()

    for d in range(1, RING):
        pc = partner(d)
        remote(idb.at[0, pc], idb.at[0, pc], idx_ss.at[0], id0_rs.at[pc], nxt).wait_recv()

    @when(has_next)
    def _():
        id_forward(0).start()

    kv_local[1].wait()
    for j in (1, 3, 2):
        wait_chunk(1, 0, partner(j))

    @when(plane <= LAST_BACK)
    def _():
        for k in range(BACKS):
            back_own(k).start()

    @when(jnp.logical_and(has_next, x != 0))
    def _():
        forward(1, 0, 0).start()

    def f_event(n):
        if n < 5:
            a, slot, c = (0, 1, x) if n == 0 else (1, 1, x) if n == 1 else (0, 1, partner((1, 3, 2)[n - 2]))
        elif n < 21:
            k = n - 6
            a, slot, c = 0, 2 + k // 5, partner((0, 1, 3, 2, 0)[k % 5])
            if n % 5 == 0:
                a, slot, c = 1, n // 5, 0
        else:
            a, slot, c = 1, 1, n - 20
        if n in (0, 6, 11, 16):
            @when(plane >= slot)
            def _():
                remote(idb.at[slot], idb.at[slot], idx_ss.at[0], idz_rs.at[slot], nxt).wait_recv()

                if slot < SLOTS - 1:
                    @when(has_next)
                    def _():
                        id_forward(slot).start()

        there = plane >= slot
        if n == 5 or n > 20:
            there = jnp.logical_and(there, c != x)

        @when(there)
        def _():
            wait_chunk(a, slot, c)

        if slot < SLOTS - 1 and n != 1 and n <= 20:
            @when(jnp.logical_and(plane >= slot, has_next))
            def _():
                forward(a, slot, c).start()

        if n == 15:
            for cc in range(1, RING):
                @when(jnp.logical_and(has_next, cc != x))
                def _():
                    forward(1, 0, cc).start()

    def r_event(m):
        d, k = 1 + m // BACKS, m % BACKS
        if d <= 3:
            @when(around(d) <= LAST_BACK)
            def _():
                remote(rel.at[d - 1, k], rel.at[d - 1, k], idx_ss.at[0], rel_rs.at[d - 1, k], nxt).wait_recv()
                back_relay(d - 1, k).start()

            if d == 3:
                for e in range(2):
                    @when(plane == 1 + e)
                    def _():
                        ext_down(e, k, rel.at[2, k]).start()
        else:
            slot = 8 - d

            @when(plane >= slot)
            def _():
                wait_chunk(BACK, slot, k + 1)

                if slot > 2:
                    @when(plane != ZRING)
                    def _():
                        back_next(slot, k).start()

            if d == 4:
                @when(plane == 1)
                def _():
                    wait_ext(1, k)
                    ext_down(1, k, ext.at[1, k]).start()

            if d < 6:
                @when(plane == 0)
                def _():
                    wait_ext(d - 4, k)
                    ext_last(d - 4, k).start()

    row = lax.broadcasted_iota(jnp.int32, (ROWS, ROWS), 0)
    col = lax.broadcasted_iota(jnp.int32, (ROWS, ROWS), 1)

    def start_block(a, qb):
        @when(qb != x)
        def _():
            remote(qbuf.at[a, qb], qbuf.at[a, qb], idx_ss.at[0], q_rs.at[a, qb], nxt).wait_recv()

        @when(qb == x)
        def _():
            q_local[a].wait()

        m_sc[a, qb] = jnp.full((GROUP * ROWS, DH), NEG_BIG, jnp.float32)
        l_sc[a, qb] = jnp.zeros((GROUP * ROWS, DH), jnp.float32)
        acc_sc[a, qb] = jnp.zeros((GROUP * ROWS, DH), jnp.float32)
        if a == 0:
            qidc[qb] = jnp.transpose(jnp.broadcast_to(idb[0, qb], (ROWS, ROWS)))

    def block(a, slot, qb, c0, c1):
        query_ids = qidc[qb]
        bias = []
        for c in range(c0, c1):
            keep = query_ids == idb[slot, c]
            if slot == 0 and isinstance(qb, int) and c == qb:
                keep = keep & (row >= col)
            if slot == SLOTS - 1 and isinstance(qb, int) and c == qb:
                keep = keep & (col > row)
            bias.append(jnp.where(keep, 0.0, NEG_BIG))
        bias = jnp.concatenate(bias, axis=1)
        q_all = qbuf[a, qb]
        q4 = jnp.concatenate([q_all[:, g * DH : (g + 1) * DH] for g in range(GROUP)], axis=0)
        span = slice(c0 * ROWS, c1 * ROWS)
        keys = kvb[a, slot, 0, span, :]
        values = kvb[a, slot, 1, span, :]
        s = lax.dot_general(q4, keys, (((1,), (1,)), ((), ())), preferred_element_type=jnp.float32)
        s = s + jnp.concatenate([bias] * GROUP, axis=0)
        m_prev = m_sc[a, qb]
        m_new = jnp.maximum(m_prev, jnp.max(s, axis=1, keepdims=True))
        alpha = jnp.exp2((m_prev - m_new) * SCALE)
        p = jnp.exp2((s - jnp.concatenate([m_new] * (c1 - c0), axis=1)) * SCALE)
        part = p[:, :ROWS]
        for c in range(1, c1 - c0):
            part = part + p[:, c * ROWS : (c + 1) * ROWS]
        l_sc[a, qb] = l_sc[a, qb] * alpha + part
        acc_sc[a, qb] = acc_sc[a, qb] * alpha + jnp.dot(
            p.astype(jnp.bfloat16), values, preferred_element_type=jnp.float32
        )
        m_sc[a, qb] = m_new

    def inner(a, slot, lo, hi, c0=0):
        @when(plane >= slot)
        def _():
            def one(qb, carry):
                block(a, slot, qb, c0, RING)
                return carry

            lax.fori_loop(lo, hi, one, 0)

    def diagonal(a, lo, hi):
        for qb in range(lo, hi):
            start_block(a, qb)
            block(a, 0, qb, 0, qb + 1)

    def edge(a, lo, hi, c0=0):
        @when(plane >= SLOTS - 1)
        def _():
            for qb in range(lo, hi):
                block(a, SLOTS - 1, qb, max(qb, c0), RING)

    def first_chunk(slot, lo, hi):
        @when(plane >= slot)
        def _():
            for qb in range(lo, hi):
                block(BACK, slot, qb, 0, 1)

    def finish(a, lo, hi):
        for qb in range(lo, hi):
            out = acc_sc[a, qb] / jnp.sum(l_sc[a, qb], axis=1, keepdims=True)
            for g in range(GROUP):
                obuf[a, qb, :, g * DH : (g + 1) * DH] = out[g * ROWS : (g + 1) * ROWS].astype(jnp.bfloat16)

            @when(qb != x)
            def _():
                o_send(a, qb).start()

            @when(qb == x)
            def _():
                o_local(a).start()

    def near(lo, hi):
        @when(plane >= 1)
        def _():
            def one(qb, carry):
                block(BACK, 1, qb, lo, hi)
                return carry

            lax.fori_loop(0, RING, one, 0)

    work = {
        6: [lambda: diagonal(0, 0, 4)],
        7: [lambda: inner(0, 1, 0, 2)],
        8: [lambda: inner(0, 1, 2, 4)],
        10: [lambda: inner(0, 2, 0, 2)],
        11: [lambda: inner(0, 2, 2, 4)],
        12: [lambda: diagonal(1, 0, 2)],
        13: [lambda: diagonal(1, 2, 4)],
        15: [lambda: inner(0, 3, 0, 2)],
        16: [lambda: inner(0, 3, 2, 4)],
        18: [lambda: inner(1, 3, 0, 4)],
        19: [lambda: edge(0, 0, 4), lambda: finish(0, 0, 4)],
        20: [lambda: edge(1, 0, 4)],
        21: [lambda: inner(1, 2, 0, 4)],
        22: [lambda: near(0, 3)],
        23: [lambda: near(3, 4), lambda: finish(1, 0, 4)],
    }
    early = plane == ZRING
    late = jnp.logical_or(plane == ZRING - 1, plane == ZRING - 2)
    lags = (
        (R_EARLY, early),
        (R_LATE, late),
        (R_LAG, jnp.logical_not(jnp.logical_or(early, late))),
    )
    for n in range(F_EVENTS):
        for lag, mine in lags:
            ms = range(0, n - lag + 1) if n == 0 else (n - lag,)
            for m in ms:
                if 0 <= m < 6 * BACKS:
                    @when(mine)
                    def _():
                        r_event(m)
        f_event(n)
        for item in work.get(n, ()):
            item()

    for a in range(HEADS):
        for d in range(1, RING):
            kv_send(a, d).wait_send()
            q_send(a, d).wait_send()
            pc = partner(d)
            o_send(a, pc).wait_send()
            remote(o_dst(pc, a), o_dst(pc, a), idx_ss.at[0], o_rs.at[a, pc], nxt).wait_recv()
        o_local(a).wait()
    for d in range(1, RING):
        id_send(d).wait_send()

    @when(has_next)
    def _():
        for slot in range(SLOTS - 1):
            @when(plane >= slot)
            def _():
                id_forward(slot).wait_send()
                for c in range(RING):
                    forward(0, slot, c).wait_send()
                for c in range(RING if slot == 0 else 1):
                    forward(1, slot, c).wait_send()

    for k in range(BACKS):
        @when(plane <= LAST_BACK)
        def _():
            back_own(k).wait_send()

        for i in range(3):
            @when(around(i + 1) <= LAST_BACK)
            def _():
                back_relay(i, k).wait_send()

        for slot in (4, 3):
            @when(jnp.logical_and(plane >= slot, plane != ZRING))
            def _():
                back_next(slot, k).wait_send()

        for e in range(2):
            @when(jnp.logical_or(plane == 0, jnp.logical_or(plane == 1, plane == 1 + e)))
            def _():
                ext_down(e, k, ext.at[e, k]).wait_send()


def local(queries, keys_values, segment_ids):
    dma = pltpu.SemaphoreType.DMA
    return pl.pallas_call(
        kernel,
        out_shape=jax.ShapeDtypeStruct(queries.shape, queries.dtype),
        in_specs=[
            pl.BlockSpec(memory_space=pl.ANY),
            pl.BlockSpec(memory_space=pl.ANY),
            pl.BlockSpec(memory_space=pltpu.VMEM),
        ],
        out_specs=pl.BlockSpec(memory_space=pl.ANY),
        scratch_shapes=[
            pltpu.VMEM((HEADS, RING, ROWS, WIDE), jnp.bfloat16),
            pltpu.VMEM((HEADS, SLOTS, 2, PLANE, DH), jnp.bfloat16),
            pltpu.VMEM((3, BACKS, 2, ROWS, DH), jnp.bfloat16),
            pltpu.VMEM((SLOTS, RING, 1, ROWS), jnp.int32),
            pltpu.VMEM((RING, ROWS, ROWS), jnp.int32),
            pltpu.VMEM((HEADS, RING, GROUP * ROWS, DH), jnp.float32),
            pltpu.VMEM((HEADS, RING, GROUP * ROWS, DH), jnp.float32),
            pltpu.VMEM((HEADS, RING, GROUP * ROWS, DH), jnp.float32),
            pltpu.VMEM((HEADS, RING, ROWS, WIDE), jnp.bfloat16),
            dma((3 * HEADS,)),
            dma((HEADS, RING - 1)),
            dma((HEADS, SLOTS, RING)),
            dma((HEADS, SLOTS - 1, RING)),
            dma((HEADS, RING - 1)),
            dma((HEADS, RING)),
            dma((RING - 1,)),
            dma((RING,)),
            dma((SLOTS - 1,)),
            dma((SLOTS,)),
            dma((HEADS, RING)),
            dma((HEADS, RING)),
            dma((BACKS,)),
            dma((3, BACKS)),
            dma((3, BACKS)),
            dma((2, BACKS)),
            pltpu.VMEM((2, BACKS, 2, ROWS, DH), jnp.bfloat16),
            dma((2, BACKS)),
            dma((2, BACKS)),
        ],
        compiler_params=pltpu.CompilerParams(collective_id=0, has_side_effects=True),
        name="window_attention",
    )(queries, keys_values, segment_ids.reshape(1, ROWS))


def solution(mesh):
    return jax.shard_map(
        local,
        mesh=mesh,
        in_specs=(P(("rep", "seq"), None), P(None, ("rep", "seq"), None), P(("rep", "seq"))),
        out_specs=P(("rep", "seq"), None),
        check_vma=False,
    )
```

time: 72.6 us -> 68 us (0.937)
  Pallas kernels: 69.8 us -> 65.6 us
    pallas_call x1, Pallas kernels: 69.8 us -> 65.6 us  [local(): pl.pallas_call(kernel, out_shape=jax.ShapeDtypeStruct(queries.shape, quer...]
where the time goes in v2:
time: 68 us; the launch traced here: 67.9 us
  Pallas kernels  65.6 us (96%)
  local copies, waits for them, and re-layouts  2.29 us (3%)
    pallas_call x1, Pallas kernels, local(): pl.pallas_call(kernel, out_shape=jax.ShapeDtypeStruct(queries.shape, quer...  65.6 us
    unnamed x1, local copies, waits for them, and re-layouts  2.29 us

profile of v2, /device:TPU:24, one launch (start us, length us, event | category | flops | bytes accessed | tf_op | source)
XLA Modules:
  0.0 67.9 jit_solution(5799446420554329966)
XLA Ops:
  0.0 65.6 %window_attention.1 = bf16[128,4096]{1,0:T(8,128)(2,1)} custom-call(bf16[128,4096]{1,0:T(8,128)(2,1)} %q_hbm.1, bf16[2,128,1024]{2,1,0:T(8,128)(2,1)} %kv_hbm.1, s32[1,128]{1,0:T(1,128)} %bitcast.1), custom_call_target="tpu_custom_call" | custom-call | tf_op jit(solution)/shard_map/window_attention/pallas_call | solution.py:481
  65.6 2.3 %copy.5 = bf16[128,4096]{1,0:T(8,128)(2,1)} copy(bf16[128,4096]{1,0:T(8,128)(2,1)} %window_attention.1) | data formatting | bytes 2097152

commit v3 on v2

--- a/solution.py
+++ b/solution.py
@@ -28,16 +28,16 @@
 BACKS = RING - 1
 LAST_BACK = PLANES - 3
 F_EVENTS = 24
-R_LAG = 4
-R_EARLY = 4
-R_LATE = 4
+R_LAG = 10
+R_EARLY = 8
+R_EVENTS = 4 * BACKS
 
 
 def kernel(
     q_hbm, kv_hbm, id_in, o_hbm,
     qbuf, kvb, rel, idb, qidc, m_sc, l_sc, acc_sc, obuf,
     loc_sem, kvx_ss, kv_rs, z_ss, qx_ss, q_rs, idx_ss, id0_rs, idz_ss, idz_rs, o_ss, o_rs,
-    back_ss, rel_ss, rel_rs, rz_ss, ext, ext_ss, ext_rs,
+    back_ss, rel_ss, rel_rs, rz_ss, side_ss,
 ):
     me = lax.axis_index("seq")
     x = lax.rem(me, RING)
@@ -52,8 +52,8 @@
     def around(k):
         return half * ZRING + lax.rem(z + k, ZRING)
 
-    down = around(ZRING - 1) * RING + x
-    up = around(1) * RING + x
+    third = around(3)
+    relay = around(ZRING - 3) * RING + x
 
     def partner(d):
         return lax.rem(x + d, RING)
@@ -92,10 +92,9 @@
     idb[0, x] = id_in[...]
 
     barrier = pltpu.get_barrier_semaphore()
-    third = around(3)
     for d in range(1, RING):
         signal(barrier, ring_base + partner(d))
-    signal(barrier, up)
+    signal(barrier, third * RING + x)
 
     @when(plane > 0)
     def _():
@@ -118,7 +117,13 @@
     def _():
         signal(barrier, nxt)
 
-    targets = (has_next, third <= LAST_BACK, jnp.logical_and(plane >= 3, plane != ZRING))
+    @when(plane == ZRING - 1)
+    def _():
+        signal(barrier, RING + x)
+        signal(barrier, 2 * RING + x)
+
+    helper = jnp.logical_or(plane == 1, plane == 2)
+    targets = (has_next, third <= LAST_BACK, jnp.logical_and(plane >= 3, plane != ZRING), helper)
     count = jnp.int32(RING)
     for target in targets:
         count = count + jnp.where(target, 1, 0)
@@ -148,31 +153,25 @@
         remote(chunk(a, slot, c), chunk(a, slot, c), kvx_ss.at[0, 0], kv_rs.at[a, slot, c], nxt).wait_recv()
 
     def back_own(k):
-        return remote(chunk(BACK, 0, k + 1), rel.at[0, k], back_ss.at[k], rel_rs.at[0, k], down)
-
-    def back_relay(i, k):
-        if i < 2:
-            return remote(rel.at[i, k], rel.at[i + 1, k], rel_ss.at[i, k], rel_rs.at[i + 1, k], down)
+        return remote(chunk(BACK, 0, k + 1), rel.at[k], back_ss.at[k], rel_rs.at[k], relay)
+
+    def back_relay(k):
         over = jnp.maximum(third - (PLANES - SLOTS), 0)
         slot = SLOTS - 1 - over
         first = jnp.minimum(third + SLOTS - 1, PLANES - 1) * RING + x
-        return remote(rel.at[i, k], chunk(BACK, slot, k + 1), rel_ss.at[i, k], kv_rs.at[BACK, slot, k + 1], first)
+        return remote(rel.at[k], chunk(BACK, slot, k + 1), rel_ss.at[k], kv_rs.at[BACK, slot, k + 1], first)
+
+    def back_side(k):
+        slot = 4 - plane
+        return remote(
+            rel.at[k], chunk(BACK, slot, k + 1), side_ss.at[k], kv_rs.at[BACK, slot, k + 1], (ZRING - 1) * RING + x
+        )
 
     def back_next(slot, k):
         return remote(
             chunk(BACK, slot, k + 1), chunk(BACK, slot - 1, k + 1),
-            rz_ss.at[slot - 3, k], kv_rs.at[BACK, slot - 1, k + 1], prv,
+            rz_ss.at[slot - 2, k], kv_rs.at[BACK, slot - 1, k + 1], prv,
         )
-
-    def ext_down(e, k, src):
-        return remote(src, ext.at[e, k], ext_ss.at[e, k], ext_rs.at[e, k], down)
-
-    def ext_last(e, k):
-        slot = 3 - e
-        return remote(ext.at[e, k], chunk(BACK, slot, k + 1), ext_ss.at[e, k], kv_rs.at[BACK, slot, k + 1], down)
-
-    def wait_ext(e, k):
-        remote(ext.at[e, k], ext.at[e, k], idx_ss.at[0], ext_rs.at[e, k], nxt).wait_recv()
 
     def o_send(a, qb):
         return remote(obuf.at[a, qb], o_dst(x, a), o_ss.at[a, qb], o_rs.at[a, x], ring_base + qb)
@@ -182,8 +181,11 @@
 
     @when(has_next)
     def _():
-        for a in range(HEADS):
-            own_forward(a).start()
+        own_forward(0).start()
+
+    @when(jnp.logical_and(has_next, jnp.logical_or(plane != ZRING - 1, x == 0)))
+    def _():
+        own_forward(1).start()
 
     for d in range(1, RING):
         id_send(d).start()
@@ -210,18 +212,26 @@
     def _():
         id_forward(0).start()
 
+    def back_start(c):
+        @when(jnp.logical_and(plane <= LAST_BACK, c > 0))
+        def _():
+            back_own(c - 1).start()
+
     kv_local[1].wait()
+    back_start(x)
     for j in (1, 3, 2):
         wait_chunk(1, 0, partner(j))
-
-    @when(plane <= LAST_BACK)
-    def _():
-        for k in range(BACKS):
-            back_own(k).start()
+        back_start(partner(j))
 
     @when(jnp.logical_and(has_next, x != 0))
     def _():
         forward(1, 0, 0).start()
+
+    rest_late = jnp.logical_and(has_next, jnp.logical_and(plane != ZRING - 1, plane != ZRING))
+    for cc in range(1, RING):
+        @when(jnp.logical_and(plane == ZRING, cc != x))
+        def _():
+            forward(1, 0, cc).start()
 
     def f_event(n):
         if n < 5:
@@ -244,8 +254,12 @@
                         id_forward(slot).start()
 
         there = plane >= slot
-        if n == 5 or n > 20:
+        if n == 1:
+            there = jnp.logical_and(there, jnp.logical_or(plane != ZRING, x == 0))
+        if n == 5:
             there = jnp.logical_and(there, c != x)
+        if n > 20:
+            there = jnp.logical_and(there, jnp.logical_or(plane == ZRING, c != x))
 
         @when(there)
         def _():
@@ -258,46 +272,34 @@
 
         if n == 15:
             for cc in range(1, RING):
-                @when(jnp.logical_and(has_next, cc != x))
+                @when(jnp.logical_and(rest_late, cc != x))
                 def _():
                     forward(1, 0, cc).start()
 
     def r_event(m):
-        d, k = 1 + m // BACKS, m % BACKS
-        if d <= 3:
-            @when(around(d) <= LAST_BACK)
-            def _():
-                remote(rel.at[d - 1, k], rel.at[d - 1, k], idx_ss.at[0], rel_rs.at[d - 1, k], nxt).wait_recv()
-                back_relay(d - 1, k).start()
-
-            if d == 3:
-                for e in range(2):
-                    @when(plane == 1 + e)
-                    def _():
-                        ext_down(e, k, rel.at[2, k]).start()
+        step, k = m // BACKS, m % BACKS
+        if step == 0:
+            @when(third <= LAST_BACK)
+            def _():
+                remote(rel.at[k], rel.at[k], idx_ss.at[0], rel_rs.at[k], nxt).wait_recv()
+                back_relay(k).start()
+
+            @when(helper)
+            def _():
+                back_side(k).start()
         else:
-            slot = 8 - d
+            slot = SLOTS - step
+            on = plane != ZRING
+            if slot == 2:
+                on = plane == ZRING + 1
 
             @when(plane >= slot)
             def _():
                 wait_chunk(BACK, slot, k + 1)
 
-                if slot > 2:
-                    @when(plane != ZRING)
-                    def _():
-                        back_next(slot, k).start()
-
-            if d == 4:
-                @when(plane == 1)
+                @when(on)
                 def _():
-                    wait_ext(1, k)
-                    ext_down(1, k, ext.at[1, k]).start()
-
-            if d < 6:
-                @when(plane == 0)
-                def _():
-                    wait_ext(d - 4, k)
-                    ext_last(d - 4, k).start()
+                    back_next(slot, k).start()
 
     row = lax.broadcasted_iota(jnp.int32, (ROWS, ROWS), 0)
     col = lax.broadcasted_iota(jnp.int32, (ROWS, ROWS), 1)
@@ -317,62 +319,56 @@
         if a == 0:
             qidc[qb] = jnp.transpose(jnp.broadcast_to(idb[0, qb], (ROWS, ROWS)))
 
-    def block(a, slot, qb, c0, c1):
-        query_ids = qidc[qb]
-        bias = []
-        for c in range(c0, c1):
-            keep = query_ids == idb[slot, c]
-            if slot == 0 and isinstance(qb, int) and c == qb:
-                keep = keep & (row >= col)
-            if slot == SLOTS - 1 and isinstance(qb, int) and c == qb:
-                keep = keep & (col > row)
-            bias.append(jnp.where(keep, 0.0, NEG_BIG))
-        bias = jnp.concatenate(bias, axis=1)
-        q_all = qbuf[a, qb]
-        q4 = jnp.concatenate([q_all[:, g * DH : (g + 1) * DH] for g in range(GROUP)], axis=0)
-        span = slice(c0 * ROWS, c1 * ROWS)
-        keys = kvb[a, slot, 0, span, :]
-        values = kvb[a, slot, 1, span, :]
-        s = lax.dot_general(q4, keys, (((1,), (1,)), ((), ())), preferred_element_type=jnp.float32)
-        s = s + jnp.concatenate([bias] * GROUP, axis=0)
-        m_prev = m_sc[a, qb]
-        m_new = jnp.maximum(m_prev, jnp.max(s, axis=1, keepdims=True))
-        alpha = jnp.exp2((m_prev - m_new) * SCALE)
-        p = jnp.exp2((s - jnp.concatenate([m_new] * (c1 - c0), axis=1)) * SCALE)
-        part = p[:, :ROWS]
-        for c in range(1, c1 - c0):
-            part = part + p[:, c * ROWS : (c + 1) * ROWS]
-        l_sc[a, qb] = l_sc[a, qb] * alpha + part
-        acc_sc[a, qb] = acc_sc[a, qb] * alpha + jnp.dot(
-            p.astype(jnp.bfloat16), values, preferred_element_type=jnp.float32
-        )
-        m_sc[a, qb] = m_new
-
-    def inner(a, slot, lo, hi, c0=0):
+    def blocks(a, slot, spans):
+        ids = [idb[slot, c] for c in range(RING)]
+        state, scores = [], []
+        for qb, c0, c1 in spans:
+            query_ids = qidc[qb]
+            bias = []
+            for c in range(c0, c1):
+                keep = query_ids == ids[c]
+                if slot == 0 and isinstance(qb, int) and c == qb:
+                    keep = keep & (row >= col)
+                if slot == SLOTS - 1 and isinstance(qb, int) and c == qb:
+                    keep = keep & (col > row)
+                bias.append(jnp.where(keep, 0.0, NEG_BIG))
+            bias = jnp.concatenate(bias, axis=1)
+            q_all = qbuf[a, qb]
+            q4 = jnp.concatenate([q_all[:, g * DH : (g + 1) * DH] for g in range(GROUP)], axis=0)
+            keys = kvb[a, slot, 0, c0 * ROWS : c1 * ROWS, :]
+            state.append((m_sc[a, qb], l_sc[a, qb], acc_sc[a, qb]))
+            s = lax.dot_general(q4, keys, (((1,), (1,)), ((), ())), preferred_element_type=jnp.float32)
+            scores.append(s + jnp.concatenate([bias] * GROUP, axis=0))
+        new = []
+        for (qb, c0, c1), (m_prev, l_prev, acc_prev), s in zip(spans, state, scores):
+            values = kvb[a, slot, 1, c0 * ROWS : c1 * ROWS, :]
+            m_new = jnp.maximum(m_prev, jnp.max(s, axis=1, keepdims=True))
+            alpha = jnp.exp2((m_prev - m_new) * SCALE)
+            p = jnp.exp2((s - jnp.concatenate([m_new] * (c1 - c0), axis=1)) * SCALE)
+            part = p[:, :ROWS]
+            for c in range(1, c1 - c0):
+                part = part + p[:, c * ROWS : (c + 1) * ROWS]
+            acc = acc_prev * alpha + jnp.dot(p.astype(jnp.bfloat16), values, preferred_element_type=jnp.float32)
+            new.append((m_new, l_prev * alpha + part, acc))
+        for (qb, _, _), (m_new, l_new, acc) in zip(spans, new):
+            m_sc[a, qb] = m_new
+            l_sc[a, qb] = l_new
+            acc_sc[a, qb] = acc
+
+    def inner(a, slot, lo, hi):
         @when(plane >= slot)
         def _():
-            def one(qb, carry):
-                block(a, slot, qb, c0, RING)
-                return carry
-
-            lax.fori_loop(lo, hi, one, 0)
+            blocks(a, slot, [(qb, 0, RING) for qb in range(lo, hi)])
 
     def diagonal(a, lo, hi):
         for qb in range(lo, hi):
             start_block(a, qb)
-            block(a, 0, qb, 0, qb + 1)
-
-    def edge(a, lo, hi, c0=0):
+        blocks(a, 0, [(qb, 0, qb + 1) for qb in range(lo, hi)])
+
+    def edge(a, lo, hi):
         @when(plane >= SLOTS - 1)
         def _():
-            for qb in range(lo, hi):
-                block(a, SLOTS - 1, qb, max(qb, c0), RING)
-
-    def first_chunk(slot, lo, hi):
-        @when(plane >= slot)
-        def _():
-            for qb in range(lo, hi):
-                block(BACK, slot, qb, 0, 1)
+            blocks(a, SLOTS - 1, [(qb, qb, RING) for qb in range(lo, hi)])
 
     def finish(a, lo, hi):
         for qb in range(lo, hi):
@@ -391,11 +387,12 @@
     def near(lo, hi):
         @when(plane >= 1)
         def _():
-            def one(qb, carry):
-                block(BACK, 1, qb, lo, hi)
+            def one(k, carry):
+                qb = 2 * k
+                blocks(BACK, 1, [(qb, lo, hi), (qb + 1, lo, hi)])
                 return carry
 
-            lax.fori_loop(0, RING, one, 0)
+            lax.fori_loop(0, RING // 2, one, 0)
 
     work = {
         6: [lambda: diagonal(0, 0, 4)],
@@ -403,10 +400,9 @@
         8: [lambda: inner(0, 1, 2, 4)],
         10: [lambda: inner(0, 2, 0, 2)],
         11: [lambda: inner(0, 2, 2, 4)],
-        12: [lambda: diagonal(1, 0, 2)],
-        13: [lambda: diagonal(1, 2, 4)],
-        15: [lambda: inner(0, 3, 0, 2)],
-        16: [lambda: inner(0, 3, 2, 4)],
+        12: [lambda: diagonal(1, 0, 4)],
+        14: [lambda: inner(0, 3, 0, 2)],
+        15: [lambda: inner(0, 3, 2, 4)],
         18: [lambda: inner(1, 3, 0, 4)],
         19: [lambda: edge(0, 0, 4), lambda: finish(0, 0, 4)],
         20: [lambda: edge(1, 0, 4)],
@@ -415,19 +411,13 @@
         23: [lambda: near(3, 4), lambda: finish(1, 0, 4)],
     }
     early = plane == ZRING
-    late = jnp.logical_or(plane == ZRING - 1, plane == ZRING - 2)
-    lags = (
-        (R_EARLY, early),
-        (R_LATE, late),
-        (R_LAG, jnp.logical_not(jnp.logical_or(early, late))),
-    )
     for n in range(F_EVENTS):
-        for lag, mine in lags:
-            ms = range(0, n - lag + 1) if n == 0 else (n - lag,)
-            for m in ms:
-                if 0 <= m < 6 * BACKS:
-                    @when(mine)
-                    def _():
+        for mine, first, rest in ((early, 4, 10), (jnp.logical_not(early), 10, 10)):
+            ms = [m for m in range(R_EVENTS) if m + (first if m < BACKS else rest) == n]
+            if ms:
+                @when(mine)
+                def _():
+                    for m in ms:
                         r_event(m)
         f_event(n)
         for item in work.get(n, ()):
@@ -452,28 +442,34 @@
                 id_forward(slot).wait_send()
                 for c in range(RING):
                     forward(0, slot, c).wait_send()
-                for c in range(RING if slot == 0 else 1):
-                    forward(1, slot, c).wait_send()
+                forward(1, slot, 0).wait_send()
+                if slot == 0:
+                    @when(plane != ZRING - 1)
+                    def _():
+                        for c in range(1, RING):
+                            forward(1, slot, c).wait_send()
 
     for k in range(BACKS):
         @when(plane <= LAST_BACK)
         def _():
             back_own(k).wait_send()
 
-        for i in range(3):
-            @when(around(i + 1) <= LAST_BACK)
-            def _():
-                back_relay(i, k).wait_send()
-
-        for slot in (4, 3):
-            @when(jnp.logical_and(plane >= slot, plane != ZRING))
+        @when(third <= LAST_BACK)
+        def _():
+            back_relay(k).wait_send()
+
+        @when(helper)
+        def _():
+            back_side(k).wait_send()
+
+        for slot in (4, 3, 2):
+            on = plane != ZRING
+            if slot == 2:
+                on = plane == ZRING + 1
+
+            @when(jnp.logical_and(plane >= slot, on))
             def _():
                 back_next(slot, k).wait_send()
-
-        for e in range(2):
-            @when(jnp.logical_or(plane == 0, jnp.logical_or(plane == 1, plane == 1 + e)))
-            def _():
-                ext_down(e, k, ext.at[e, k]).wait_send()
 
 
 def local(queries, keys_values, segment_ids):
@@ -482,15 +478,15 @@
         kernel,
         out_shape=jax.ShapeDtypeStruct(queries.shape, queries.dtype),
         in_specs=[
-            pl.BlockSpec(memory_space=pl.ANY),
-            pl.BlockSpec(memory_space=pl.ANY),
+            pl.BlockSpec(memory_space=pltpu.HBM),
+            pl.BlockSpec(memory_space=pltpu.HBM),
             pl.BlockSpec(memory_space=pltpu.VMEM),
         ],
         out_specs=pl.BlockSpec(memory_space=pl.ANY),
         scratch_shapes=[
             pltpu.VMEM((HEADS, RING, ROWS, WIDE), jnp.bfloat16),
             pltpu.VMEM((HEADS, SLOTS, 2, PLANE, DH), jnp.bfloat16),
-            pltpu.VMEM((3, BACKS, 2, ROWS, DH), jnp.bfloat16),
+            pltpu.VMEM((BACKS, 2, ROWS, DH), jnp.bfloat16),
             pltpu.VMEM((SLOTS, RING, 1, ROWS), jnp.int32),
             pltpu.VMEM((RING, ROWS, ROWS), jnp.int32),
             pltpu.VMEM((HEADS, RING, GROUP * ROWS, DH), jnp.float32),
@@ -510,16 +506,18 @@
             dma((HEADS, RING)),
             dma((HEADS, RING)),
             dma((BACKS,)),
+            dma((BACKS,)),
+            dma((BACKS,)),
             dma((3, BACKS)),
-            dma((3, BACKS)),
-            dma((2, BACKS)),
-            pltpu.VMEM((2, BACKS, 2, ROWS, DH), jnp.bfloat16),
-            dma((2, BACKS)),
-            dma((2, BACKS)),
+            dma((BACKS,)),
         ],
-        compiler_params=pltpu.CompilerParams(collective_id=0, has_side_effects=True),
+        compiler_params=pltpu.CompilerParams(collective_id=0, has_side_effects=True, vmem_limit_bytes=32 * 1024 * 1024),
         name="window_attention",
-    )(queries, keys_values, segment_ids.reshape(1, ROWS))
+    )(
+        pltpu.with_memory_space_constraint(queries, pltpu.HBM),
+        pltpu.with_memory_space_constraint(keys_values, pltpu.HBM),
+        segment_ids.reshape(1, ROWS),
+    )
 
 
 def solution(mesh):

time: 68 us -> 62.7 us (0.922)
  Pallas kernels: 65.6 us -> 61 us
    pallas_call x1, Pallas kernels: 65.6 us -> 61 us  [local(): pl.pallas_call(kernel, out_shape=jax.ShapeDtypeStruct(queries.shape, quer...]
    unnamed x1 -> x3, local copies, waits for them, and re-layouts: 2.29 us -> 1.63 us
where the time goes in v3:
time: 62.7 us; the launch traced here: 62.6 us
  Pallas kernels  61 us (97%)
  local copies, waits for them, and re-layouts  1.63 us (3%)
    pallas_call x1, Pallas kernels, local(): pl.pallas_call(kernel, out_shape=jax.ShapeDtypeStruct(queries.shape, quer...  61 us
    unnamed x3, local copies, waits for them, and re-layouts  1.63 us

profile of v3, /device:TPU:24, one launch (start us, length us, event | category | flops | bytes accessed | tf_op | source)
XLA Modules:
  0.0 62.6 jit_solution(13715254254710101528)
XLA Ops:
  0.0 0.0 copy-start
  0.0 0.7 %copy-done = s32[128]{0:T(128)S(1)} copy-done((s32[128]{0:T(128)S(1)}, s32[128]{0:T(128)}, u32[]{:S(2)}) %copy-start) | copy-done | bytes 536
  0.7 61.0 %window_attention.1 = bf16[128,4096]{1,0:T(8,128)(2,1)S(1)} custom-call(bf16[128,4096]{1,0:T(8,128)(2,1)} %q_hbm.1, bf16[2,128,1024]{2,1,0:T(8,128)(2,1)} %kv_hbm.1, s32[1,128]{1,0:T(1,128)S(1)} %bitcast.1), custom_call_target="tpu_custom_call" | custom-call | tf_op jit(solution)/shard_map/window_attention/pallas_call | solution.py:477
  61.6 1.0 %copy.5 = bf16[128,4096]{1,0:T(8,128)(2,1)} copy(bf16[128,4096]{1,0:T(8,128)(2,1)S(1)} %window_attention.1) | data formatting | bytes 2097152
Async XLA Ops:
  0.0 0.7 %copy-start = (s32[128]{0:T(128)S(1)}, s32[128]{0:T(128)}, u32[]{:S(2)}) copy-start(s32[128]{0:T(128)} %param.5) | copy-start | bytes 1540

commit v4 on v3

--- a/solution.py
+++ b/solution.py
@@ -384,15 +384,10 @@
             def _():
                 o_local(a).start()
 
-    def near(lo, hi):
+    def near(lo, hi, first=0, last=RING):
         @when(plane >= 1)
         def _():
-            def one(k, carry):
-                qb = 2 * k
-                blocks(BACK, 1, [(qb, lo, hi), (qb + 1, lo, hi)])
-                return carry
-
-            lax.fori_loop(0, RING // 2, one, 0)
+            blocks(BACK, 1, [(qb, lo, hi) for qb in range(first, last)])
 
     work = {
         6: [lambda: diagonal(0, 0, 4)],
@@ -406,9 +401,12 @@
         18: [lambda: inner(1, 3, 0, 4)],
         19: [lambda: edge(0, 0, 4), lambda: finish(0, 0, 4)],
         20: [lambda: edge(1, 0, 4)],
-        21: [lambda: inner(1, 2, 0, 4)],
-        22: [lambda: near(0, 3)],
-        23: [lambda: near(3, 4), lambda: finish(1, 0, 4)],
+        21: [lambda: inner(1, 2, 0, 2)],
+        22: [lambda: near(0, 3, 0, 2)],
+        23: [
+            lambda: near(3, 4, 0, 2), lambda: finish(1, 0, 2),
+            lambda: inner(1, 2, 2, 4), lambda: near(0, 4, 2, 4), lambda: finish(1, 2, 4),
+        ],
     }
     early = plane == ZRING
     for n in range(F_EVENTS):

time: 62.7 us -> 61.9 us (0.987)
  Pallas kernels: 61 us -> 59.8 us
    pallas_call x1, Pallas kernels: 61 us -> 59.8 us  [local(): pl.pallas_call(kernel, out_shape=jax.ShapeDtypeStruct(queries.shape, quer...]
where the time goes in v4:
time: 61.9 us; the launch traced here: 61.4 us
  Pallas kernels  59.8 us (97%)
  local copies, waits for them, and re-layouts  1.63 us (3%)
    pallas_call x1, Pallas kernels, local(): pl.pallas_call(kernel, out_shape=jax.ShapeDtypeStruct(queries.shape, quer...  59.8 us
    unnamed x3, local copies, waits for them, and re-layouts  1.63 us

profile of v4, /device:TPU:24, one launch (start us, length us, event | category | flops | bytes accessed | tf_op | source)
XLA Modules:
  0.0 61.4 jit_solution(18151002319048061305)
XLA Ops:
  0.0 0.0 copy-start
  0.0 0.7 %copy-done = s32[128]{0:T(128)S(1)} copy-done((s32[128]{0:T(128)S(1)}, s32[128]{0:T(128)}, u32[]{:S(2)}) %copy-start) | copy-done | bytes 536
  0.7 59.8 %window_attention.1 = bf16[128,4096]{1,0:T(8,128)(2,1)S(1)} custom-call(bf16[128,4096]{1,0:T(8,128)(2,1)} %q_hbm.1, bf16[2,128,1024]{2,1,0:T(8,128)(2,1)} %kv_hbm.1, s32[1,128]{1,0:T(1,128)S(1)} %bitcast.1), custom_call_target="tpu_custom_call" | custom-call | tf_op jit(solution)/shard_map/window_attention/pallas_call | solution.py:475
  60.4 1.0 %copy.5 = bf16[128,4096]{1,0:T(8,128)(2,1)} copy(bf16[128,4096]{1,0:T(8,128)(2,1)S(1)} %window_attention.1) | data formatting | bytes 2097152
Async XLA Ops:
  0.0 0.7 %copy-start = (s32[128]{0:T(128)S(1)}, s32[128]{0:T(128)}, u32[]{:S(2)}) copy-start(s32[128]{0:T(128)} %param.5) | copy-start | bytes 1540

commit v5 on v4

--- a/solution.py
+++ b/solution.py
@@ -85,42 +85,43 @@
     def when(cond):
         return pl.when(cond)
 
+    barrier = pltpu.get_barrier_semaphore()
+
+    @when(plane > 0)
+    def _():
+        signal(barrier, prv)
+
+    for d in range(1, RING):
+        signal(barrier, ring_base + partner(d))
+    signal(barrier, third * RING + x)
+
+    def last_relay(source):
+        h = source // ZRING
+        return (h * ZRING + lax.rem(source + ZRING - 3, ZRING)) * RING + x
+
+    @when(plane >= SLOTS - 1)
+    def _():
+        signal(barrier, last_relay(plane - (SLOTS - 1)))
+
+    @when(plane == PLANES - 1)
+    def _():
+        signal(barrier, last_relay(PLANES - 4))
+        signal(barrier, last_relay(PLANES - 3))
+
+    @when(jnp.logical_and(jnp.logical_and(plane >= 2, plane != ZRING - 1), has_next))
+    def _():
+        signal(barrier, nxt)
+
+    @when(plane == ZRING - 1)
+    def _():
+        signal(barrier, RING + x)
+        signal(barrier, 2 * RING + x)
+
     kv_local = [pltpu.make_async_copy(kv_src(x, a), chunk(a, 0, x), loc_sem.at[a]) for a in range(HEADS)]
     q_local = [pltpu.make_async_copy(q_src(x, a), qbuf.at[a, x], loc_sem.at[HEADS + a]) for a in range(HEADS)]
     for cp in kv_local + q_local:
         cp.start()
     idb[0, x] = id_in[...]
-
-    barrier = pltpu.get_barrier_semaphore()
-    for d in range(1, RING):
-        signal(barrier, ring_base + partner(d))
-    signal(barrier, third * RING + x)
-
-    @when(plane > 0)
-    def _():
-        signal(barrier, prv)
-
-    def last_relay(source):
-        h = source // ZRING
-        return (h * ZRING + lax.rem(source + ZRING - 3, ZRING)) * RING + x
-
-    @when(plane >= SLOTS - 1)
-    def _():
-        signal(barrier, last_relay(plane - (SLOTS - 1)))
-
-    @when(plane == PLANES - 1)
-    def _():
-        signal(barrier, last_relay(PLANES - 4))
-        signal(barrier, last_relay(PLANES - 3))
-
-    @when(jnp.logical_and(jnp.logical_and(plane >= 2, plane != ZRING - 1), has_next))
-    def _():
-        signal(barrier, nxt)
-
-    @when(plane == ZRING - 1)
-    def _():
-        signal(barrier, RING + x)
-        signal(barrier, 2 * RING + x)
 
     helper = jnp.logical_or(plane == 1, plane == 2)
     targets = (has_next, third <= LAST_BACK, jnp.logical_and(plane >= 3, plane != ZRING), helper)
@@ -410,8 +411,12 @@
     }
     early = plane == ZRING
     for n in range(F_EVENTS):
-        for mine, first, rest in ((early, 4, 10), (jnp.logical_not(early), 10, 10)):
-            ms = [m for m in range(R_EVENTS) if m + (first if m < BACKS else rest) == n]
+        for mine, ticks in (
+            (early, [4, 5, 6] + [18] * 6 + [21] * 3),
+            (plane == ZRING + 1, [m + 10 for m in range(R_EVENTS)]),
+            ((plane != ZRING) & (plane != ZRING + 1), [m + 10 for m in range(9)] + [21] * 3),
+        ):
+            ms = [m for m in range(R_EVENTS) if ticks[m] == n]
             if ms:
                 @when(mine)
                 def _():

time: 61.9 us -> 62.1 us (level)
  no operation moved by 1% of the time
where the time goes in v5:
time: 62.1 us; the launch traced here: 61.4 us
  Pallas kernels  59.7 us (96%)
  local copies, waits for them, and re-layouts  1.63 us (3%)
    pallas_call x1, Pallas kernels, local(): pl.pallas_call(kernel, out_shape=jax.ShapeDtypeStruct(queries.shape, quer...  59.7 us
    unnamed x3, local copies, waits for them, and re-layouts  1.63 us

profile of v5, /device:TPU:24, one launch (start us, length us, event | category | flops | bytes accessed | tf_op | source)
XLA Modules:
  0.0 61.4 jit_solution(2587398999572076311)
XLA Ops:
  0.0 0.0 copy-start
  0.0 0.7 %copy-done = s32[128]{0:T(128)S(1)} copy-done((s32[128]{0:T(128)S(1)}, s32[128]{0:T(128)}, u32[]{:S(2)}) %copy-start) | copy-done | bytes 536
  0.7 59.7 %window_attention.1 = bf16[128,4096]{1,0:T(8,128)(2,1)S(1)} custom-call(bf16[128,4096]{1,0:T(8,128)(2,1)} %q_hbm.1, bf16[2,128,1024]{2,1,0:T(8,128)(2,1)} %kv_hbm.1, s32[1,128]{1,0:T(1,128)S(1)} %bitcast.1), custom_call_target="tpu_custom_call" | custom-call | tf_op jit(solution)/shard_map/window_attention/pallas_call | solution.py:480
  60.4 1.0 %copy.5 = bf16[128,4096]{1,0:T(8,128)(2,1)} copy(bf16[128,4096]{1,0:T(8,128)(2,1)S(1)} %window_attention.1) | data formatting | bytes 2097152
Async XLA Ops:
  0.0 0.7 %copy-start = (s32[128]{0:T(128)S(1)}, s32[128]{0:T(128)}, u32[]{:S(2)}) copy-start(s32[128]{0:T(128)} %param.5) | copy-start | bytes 1540
